TPU v7x, 256 devices: a whole 4x4x8 slice. The times are simulated.
256 devices in a mesh: row: 16 (over y, z_hi, core), col: 16 (over z_lo, x).
Axes of the slice: x: 4, y: 4, z: 8 (z_hi: 2, z_lo: 4; z = z_hi * 4 + z_lo), core: 2. Of those that a mesh axis runs over, the one named last changes fastest.
Arguments:
- fluid_data: float32 [51, 32768], P(None, ('row', 'col')), as said below
- center_data: float32 [51, 16384], P(None, ('col', 'row')), as said below
- poly_coef: float32 [48, 4], replicated, may hold values from -3 to 3
Outputs:
- fluid_motion: float32 [48, 32768], P(None, ('row', 'col'))
- center_load: float32 [48, 16384], P(None, ('col', 'row'))
Inputs may be any that keep to these rules, and one draw needn't show every extreme that they name: Rows 0 to 2 of fluid_data lie in [0, 1]; rows 3 and on are forces. Rows 0 and 1 of center_data lie in [0, 1] and row 2 lies in [-0.5, -0.02], so every center is at least 0.02 below every vertex; rows 3 and on are coefficients.
All inputs are finite; a program needn't handle non-finite values.
Results may differ from a plain program's by a relative error of at most 0.0003.
Values sent between devices are 32-bit elements; how exact they have to be, the bound alone decides.
A program may use at most 64 MiB of HBM per device.

v0:
```python
import functools

import jax
import jax.numpy as jnp
from jax import lax
from jax.experimental import pallas as pl
from jax.experimental.pallas import tpu as pltpu
from jax.sharding import PartitionSpec as P

WAVES = 64
MESH = pl.DeviceIdType.MESH
TOP = 12.404427306735432
MID = 0.6418441597071612
LOW = 0.16126480593510223


def paired(me, m, n):
    other, bit = 0, 1
    while bit < n:
        other = other + (((me // bit) % 2 + (m // bit) % 2) % 2) * bit
        bit *= 2
    return other


def dot(a, b, dims):
    return lax.dot_general(a, b, (dims, ((), ())), preferred_element_type=jnp.float32)


def split(x):
    high = x.astype(jnp.bfloat16)
    low = (x - high.astype(jnp.float32)).astype(jnp.bfloat16)
    return high, low


def body(rows, cols, side, fluid, center, poly, motion, loads, *scratch):
    fl, ce, pv, cp, chl, fhl, kh, kl, mo_out, mo_in, ld_out, ld_in, pre = scratch[:13]
    own, fs, fr, cs, cr, ms, mr, ls, lr, ps, pr = scratch[13:]
    S, T = cols // side, rows * side
    half = T // 2
    row, col = lax.axis_index("row"), lax.axis_index("col")
    my_s, my_t = col // side, (row % 2) * half + (col % side) * (rows // 2) + row // 2
    nvals = pv.shape[1]
    wf, wc = fluid.shape[1], center.shape[1]
    lanes = 128 if wf % 128 == 0 else wf
    step_rows = 32 if wc % 32 == 0 else wc

    def along_s(m):
        return {"row": row, "col": paired(my_s, m, S) * side + col % side}

    def along_t(m):
        i = paired(my_t, m, T)
        return {
            "row": (i % (rows // 2)) * 2 + i // half,
            "col": (col // side) * side + (i % half) // (rows // 2),
        }

    def copy(src, dst, send, recv, where):
        return pltpu.make_async_remote_copy(
            src_ref=src, dst_ref=dst, send_sem=send, recv_sem=recv, device_id=where, device_id_type=MESH
        )

    def send_fluid(m):
        return copy(fl.at[0], fl.at[m], fs.at[m], fr.at[m], along_s(m))

    def send_center(p):
        return copy(ce.at[0], ce.at[p], cs.at[p], cr.at[p], along_t(half if p == 1 else p - 1))

    def hand_on(p):
        q = p + half - 1
        return copy(ce.at[p], ce.at[q], cs.at[q], cr.at[q], along_t(half))

    def send_motion(m):
        return copy(mo_out.at[m], mo_in.at[m], ms.at[m], mr.at[m], along_s(m))

    def send_pre(p):
        j = p - half
        return copy(ld_out.at[p], pre.at[j], ps.at[j], pr.at[j], along_t(half))

    def send_loads(j):
        return copy(ld_out.at[j + 1], ld_in.at[j], ls.at[j], lr.at[j], along_t(j))

    def send_other():
        return copy(ld_out.at[1], ld_in.at[0], ls.at[0], lr.at[0], along_t(half))

    local = [
        pltpu.make_async_copy(center, ce.at[0], own.at[0]),
        pltpu.make_async_copy(fluid, fl.at[0], own.at[1]),
        pltpu.make_async_copy(poly, pv, own.at[2]),
    ]
    for c in local:
        c.start()
    barrier = pltpu.get_barrier_semaphore()
    for p in range(1, half + 1):
        pl.semaphore_signal(barrier, inc=1, device_id=along_t(p), device_id_type=MESH)
    for m in range(1, S):
        pl.semaphore_signal(barrier, inc=1, device_id=along_s(m), device_id_type=MESH)
    for c in local:
        c.wait()
    order_s = [1] + list(range(S - 1, 1, -1))
    pl.semaphore_wait(barrier, S - 1 + half)
    for p in range(1, half + 1):
        send_center(p).start()
    for m in order_s:
        send_fluid(m).start()

    def ready_center(r):
        places = jnp.transpose(ce[r, 0:8, :] * float(WAVES))
        for a in range(3):
            cp[r, a] = jnp.broadcast_to(places[:, a : a + 1], (wc, lanes))
        high, low = split(ce[r, 3:, :] * TOP)
        chl[r, 0:nvals] = high
        chl[r, nvals:] = low
        ld_out[r] = jnp.zeros((nvals, wc), jnp.float32)

    def ready_fluid(m):
        high, low = split(fl[m, 3:, :] * TOP)
        fhl[m, 0:nvals] = high
        fhl[m, nvals:] = low
        mo_out[m] = jnp.zeros((nvals, wf), jnp.float32)

    def values(m, r, slot):
        for h in range(wf // lanes):
            part = pl.ds(h * lanes, lanes)
            fx, fy, fz = (fl[m, a : a + 1, part] * float(WAVES) for a in range(3))
            for j in range(0, wc, step_rows):
                at = pl.ds(j, step_rows)
                dx, dy, dz = cp[r, 0, at, :] - fx, cp[r, 1, at, :] - fy, cp[r, 2, at, :] - fz
                sq = dx * dx + dy * dy + dz * dz
                inv = lax.rsqrt(sq)
                turns = sq * inv
                f = turns - jnp.round(turns)
                size = jnp.abs(f)
                rest = 0.5 - size
                q = size * rest
                value = (f * rest * inv) * ((q + MID) * q + LOW)
                high, low = split(value)
                kh[slot, at, part] = high
                kl[slot, at, part] = low

    def sums(m, r, slot):
        k_high, k_low = kh[slot], kl[slot]
        across = ((1,), (0,))
        wide = dot(chl[r], k_high, across)
        mo_out[m] += wide[:nvals] + wide[nvals:] + dot(chl[r, 0:nvals], k_low, across)
        back = ((1,), (1,))
        wide = dot(fhl[m], k_high, back)
        ld_out[r] += wide[:nvals] + wide[nvals:] + dot(fhl[m, 0:nvals], k_low, back)

    def pair(before, one, two):
        sums(*before, 1)
        values(*one, 0)
        sums(*one, 0)
        values(*two, 1)
        return two

    kh[1] = jnp.zeros((wc, wf), jnp.bfloat16)
    kl[1] = jnp.zeros((wc, wf), jnp.bfloat16)
    ready_fluid(0)
    before = (0, 0)

    for k in range(half):
        for p in (2 * k, 2 * k + 1):
            if 2 <= p <= half:
                send_center(p).wait_recv()
                hand_on(p).start()
            elif p == 1:
                send_center(p).wait_recv()
            elif p > half:
                hand_on(p - half + 1).wait_recv()
            ready_center(p)
        if k == 0:
            send_fluid(order_s[0]).wait_recv()
            ready_fluid(order_s[0])
        m = order_s[0]
        before = pair(before, (m, 2 * k), (m, 2 * k + 1))

    def middle(s, _):
        m = S - s
        send_fluid(m).wait_recv()
        ready_fluid(m)
        last_m = (m + 1) % S + (m + 1) // S

        pair((last_m, T - 1), (m, 0), (m, 1))
        send_motion(last_m).start()

        def inner(k, _):
            pair((m, 2 * k - 1), (m, 2 * k), (m, 2 * k + 1))
            return 0

        lax.fori_loop(1, half, inner, 0)
        return 0

    lax.fori_loop(1, S - 2, middle, 0)

    far = order_s[-1]
    prior = order_s[-2]
    send_fluid(far).wait_recv()
    ready_fluid(far)
    pair((prior, T - 1), (far, T - 1), (0, T - 1))
    send_motion(prior).start()

    def mixed(k, _):
        r = T - 1 - k
        pair((0, r + 1), (far, r), (0, r))
        send_pre(r + 1).start()
        return 0

    lax.fori_loop(1, half, mixed, 0)

    def finish(j):
        send_pre(half + j).wait_recv()
        ld_out[j + 1] += pre[j]
        send_loads(j).start()

    pair((0, half), (far, half - 1), (far, half - 2))
    finish(half - 1)

    def far_rest(k, _):
        r = half - 1 - 2 * k
        pair((far, r + 1), (far, r), (far, r - 1))
        return 0

    lax.fori_loop(1, half // 2, far_rest, 0)
    pair((far, 0), (0, half - 1), (0, half - 2))
    send_motion(far).start()
    finish(half - 2)

    def own_rest(k, _):
        r = half - 1 - 2 * k
        pair((0, r + 1), (0, r), (0, r - 1))
        finish(r)

        @pl.when(r > 1)
        def _():
            finish(r - 1)

        return 0

    lax.fori_loop(1, half // 2, own_rest, 0)
    send_other().start()
    sums(0, 0, 1)

    total = mo_out[0]
    affine = jnp.transpose(pv[...])
    for a in range(3):
        total = total + affine[:, a + 1 : a + 2] * fl[0, a : a + 1, :]
    total = total + affine[:, 0:1]
    for m in order_s:
        send_motion(m).wait_recv()
        total = total + mo_in[m]
    motion[...] = total
    total = ld_out[0]
    for j in range(half - 1, 0, -1):
        send_loads(j).wait_recv()
        total = total + ld_in[j]
    send_other().wait_recv()
    loads[...] = total + ld_in[0]
    for m in order_s:
        send_fluid(m).wait_send()
        send_motion(m).wait_send()
    for p in range(1, half + 1):
        send_center(p).wait_send()
    for p in range(2, half + 1):
        hand_on(p).wait_send()
        send_pre(p + half - 1).wait_send()
        send_loads(p - 1).wait_send()
    send_other().wait_send()


def per_device(rows, cols, side, fluid_data, center_data, poly_coef):
    f32, bf16 = jnp.float32, jnp.bfloat16
    S, T = cols // side, rows * side
    height, wf = fluid_data.shape
    wc = center_data.shape[1]
    n = height - 3
    lanes = 128 if wf % 128 == 0 else wf
    vmem = pl.BlockSpec(memory_space=pltpu.VMEM)
    hbm = pl.BlockSpec(memory_space=pltpu.HBM)
    sems = [pltpu.SemaphoreType.DMA((k,)) for k in (3, S, S, T, T, S, S, T // 2, T // 2, T // 2, T // 2)]
    return pl.pallas_call(
        functools.partial(body, rows, cols, side),
        out_shape=(jax.ShapeDtypeStruct((n, wf), f32), jax.ShapeDtypeStruct((n, wc), f32)),
        in_specs=[hbm] * 3,
        out_specs=(vmem, vmem),
        scratch_shapes=[
            pltpu.VMEM((S, height, wf), f32),
            pltpu.VMEM((T, height, wc), f32),
            pltpu.VMEM((4, n), f32),
            pltpu.VMEM((T, 3, wc, lanes), f32),
            pltpu.VMEM((T, 2 * n, wc), bf16),
            pltpu.VMEM((S, 2 * n, wf), bf16),
            pltpu.VMEM((2, wc, wf), bf16),
            pltpu.VMEM((2, wc, wf), bf16),
            pltpu.VMEM((S, n, wf), f32),
            pltpu.VMEM((S, n, wf), f32),
            pltpu.VMEM((T, n, wc), f32),
            pltpu.VMEM((T // 2, n, wc), f32),
            pltpu.VMEM((T // 2, n, wc), f32),
            *sems,
        ],
        compiler_params=pltpu.CompilerParams(
            collective_id=0, has_side_effects=True, vmem_limit_bytes=67_043_328
        ),
    )(fluid_data, center_data, poly_coef.T)


def solution(mesh):
    rows, cols = mesh.shape["row"], mesh.shape["col"]
    side = 2 if cols % 2 == 0 else 1
    placed = (P(None, ("row", "col")), P(None, ("col", "row")), P())
    return jax.shard_map(
        functools.partial(per_device, rows, cols, side),
        mesh=mesh,
        in_specs=placed,
        out_specs=(P(None, ("row", "col")), P(None, ("col", "row"))),
        check_vma=False,
    )
```

profile of v0, /device:TPU:32, one launch (start us, length us, event | category | flops | bytes accessed | tf_op | source)
XLA Modules:
  0.0 71.0 jit_solution(278975040995149617)
XLA Ops:
  0.6 68.4 %shard_map.50 = (f32[48,128]{1,0:T(8,128)}, f32[48,64]{1,0:T(8,128)}) custom-call(f32[51,128]{1,0:T(8,128)} %fluid.1, f32[51,64]{1,0:T(8,128)} %center.1, f32[4,48]{1,0:T(4,128)} %bitcast.1), custom_call_target="tpu_custom_call" | custom-call | tf_op jit(solution)/shard_map/pallas_call | solution.py:280
  69.0 0.0 copy-start
  69.0 1.4 %copy.7 = f32[48,128]{1,0:T(8,128)} copy(f32[48,128]{1,0:T(8,128)} %get-tuple-element.4) | data formatting | bytes 49152
  70.4 0.0 copy-done
  70.4 0.6 copy.8
Async XLA Ops:
  69.0 1.4 %copy-start = (f32[48,64]{1,0:T(8,128)S(1)}, f32[48,64]{1,0:T(8,128)}, u32[]{:S(2)}) copy-start(f32[48,64]{1,0:T(8,128)} %get-tuple-element.5) | copy-start | bytes 36868
where the time goes:
time: 71.2 us; the launch traced here: 71 us
  Pallas kernels  68.4 us (96%)
  local copies, waits for them, and re-layouts  1.96 us (3%)
    pallas_call x1, Pallas kernels, per_device(): pl.pallas_call(functools.partial(body, rows, cols, side), out_shape=(jax....  68.4 us
    unnamed x4, local copies, waits for them, and re-layouts  1.96 us

commit v1 on v0

--- a/solution.py
+++ b/solution.py
@@ -38,20 +38,23 @@
     S, T = cols // side, rows * side
     half = T // 2
     row, col = lax.axis_index("row"), lax.axis_index("col")
-    my_s, my_t = col // side, (row % 2) * half + (col % side) * (rows // 2) + row // 2
+    side = S // 2
+    my_s = ((row // 2) % 2) * side + col // side
+    my_t = (row % 2) * half + (row // 4) * 4 + col % 4
     nvals = pv.shape[1]
     wf, wc = fluid.shape[1], center.shape[1]
     lanes = 128 if wf % 128 == 0 else wf
     step_rows = 32 if wc % 32 == 0 else wc
 
     def along_s(m):
-        return {"row": row, "col": paired(my_s, m, S) * side + col % side}
+        i = paired(my_s, m, S)
+        return {"row": (row // 4) * 4 + (i // 4) * 2 + row % 2, "col": (i % 4) * 4 + col % 4}
 
     def along_t(m):
         i = paired(my_t, m, T)
         return {
-            "row": (i % (rows // 2)) * 2 + i // half,
-            "col": (col // side) * side + (i % half) // (rows // 2),
+            "row": ((i % 16) // 4) * 4 + ((row // 2) % 2) * 2 + i // 16,
+            "col": (col // 4) * 4 + i % 4,
         }
 
     def copy(src, dst, send, recv, where):

time: 71.2 us -> 59.6 us (0.84)
  the two profiles are of different devices: /device:TPU:32 before, /device:TPU:1 now
where the time goes in v1:
time: 59.6 us; the launch traced here: 59.3 us
  Pallas kernels  56.7 us (95%)
  local copies, waits for them, and re-layouts  1.96 us (3%)
  between operations  0.65 us (1%)
    pallas_call x1, Pallas kernels, per_device(): pl.pallas_call(functools.partial(body, rows, cols, side), out_shape=(jax....  56.7 us
    unnamed x4, local copies, waits for them, and re-layouts  1.96 us

profile of v1, /device:TPU:1, one launch (start us, length us, event | category | flops | bytes accessed | tf_op | source)
XLA Modules:
  0.0 59.3 jit_solution(12020883783613690811)
XLA Ops:
  0.6 56.7 %shard_map.50 = (f32[48,128]{1,0:T(8,128)}, f32[48,64]{1,0:T(8,128)}) custom-call(f32[51,128]{1,0:T(8,128)} %fluid.1, f32[51,64]{1,0:T(8,128)} %center.1, f32[4,48]{1,0:T(4,128)} %bitcast.1), custom_call_target="tpu_custom_call" | custom-call | tf_op jit(solution)/shard_map/pallas_call | solution.py:283
  57.3 0.0 copy-start
  57.3 1.4 %copy.7 = f32[48,128]{1,0:T(8,128)} copy(f32[48,128]{1,0:T(8,128)} %get-tuple-element.4) | data formatting | bytes 49152
  58.7 0.0 copy-done
  58.7 0.6 %copy.8 = f32[48,64]{1,0:T(8,128)} copy(f32[48,64]{1,0:T(8,128)S(1)} %copy-done) | data formatting | bytes 24576
Async XLA Ops:
  57.3 1.4 %copy-start = (f32[48,64]{1,0:T(8,128)S(1)}, f32[48,64]{1,0:T(8,128)}, u32[]{:S(2)}) copy-start(f32[48,64]{1,0:T(8,128)} %get-tuple-element.5) | copy-start | bytes 36868

commit v2 on v0

v2 whole, which is shorter than its diff:
```python
import functools

import jax
import jax.numpy as jnp
from jax import lax
from jax.experimental import pallas as pl
from jax.experimental.pallas import tpu as pltpu
from jax.sharding import PartitionSpec as P

WAVES = 64
MESH = pl.DeviceIdType.MESH
TOP = 12.404427306735432
MID = 0.6418441597071612
LOW = 0.16126480593510223
X, Y, Z, CORES = 4, 4, 8, 2
GROUP = 4
PLANE = (
    ((1, 0), (3, 0), (0, 1), (0, 3))
    + ((2, 2), (2, 1), (2, 3), (1, 2))
    + ((3, 2), (1, 3), (3, 1), (3, 3))
    + ((2, 0), (0, 2), (1, 1), (0, 0))
)
OWN = len(PLANE) - 1
RING = (0, 1, 7, 2, 6, 3, 5, 4)
ORDER = tuple((c, p) for c in (0, 1) for p in range(4)) + tuple((c, p) for p in (3, 2, 1, 0) for c in (2, 3))
MERGED = (0, 1)


def dot(a, b, dims):
    return lax.dot_general(a, b, (dims, ((), ())), preferred_element_type=jnp.float32)


def split(x):
    high = x.astype(jnp.bfloat16)
    low = (x - high.astype(jnp.float32)).astype(jnp.bfloat16)
    return high, low


def body(fluid, center, poly, motion, loads, *scratch):
    fl, raw, ce, pv, cp, chl, fhl, fx, kh, kl, mo, mo_in, ld, ldp, pre, ld_in, ld_other = scratch[:17]
    own, fs, fr, cs, cr, os, orr, ms, mr, ps, pr, ls, lr, qs, qr = scratch[17:]
    row, col = lax.axis_index("row"), lax.axis_index("col")
    y, z, core = row // 4, ((row // 2) % 2) * 4 + col // 4, row % 2
    x = col % 4
    n, wf, wc = motion.shape[0], fluid.shape[1], center.shape[1]
    half = n // 2
    wide = 2 * wc
    step_rows = 32

    def at(dx, dy, dz, c):
        there = (z + dz) % Z
        return {
            "row": ((y + dy) % Y) * 4 + (there // 4) * 2 + c,
            "col": (there % 4) * 4 + (x + dx) % X,
        }

    def copy(src, dst, send, recv, where):
        return pltpu.make_async_remote_copy(
            src_ref=src, dst_ref=dst, send_sem=send, recv_sem=recv, device_id=where, device_id_type=MESH
        )

    sister = 1 - core

    def minus(s, c):
        dx, dy = PLANE[s]
        return at((X - dx) % X, (Y - dy) % Y, 0, c)

    def plus(s, c):
        dx, dy = PLANE[s]
        return at(dx, dy, 0, c)

    def send_fluid(m):
        return copy(fl.at[0], fl.at[m], fs.at[m], fr.at[m], at(0, 0, (Z - RING[m]) % Z, core))

    def send_center(s):
        return copy(ce.at[OWN, core], ce.at[s, core], cs.at[s], cr.at[s], minus(s, core))

    def send_across(s):
        return copy(ce.at[OWN, core], ce.at[s, core], os.at[s], orr.at[s], minus(s, sister))

    def hand_on(s):
        return copy(ce.at[s, core], ce.at[s, core], os.at[s], orr.at[s], at(0, 0, 0, sister))

    def from_other(s):
        return copy(ce.at[s, sister], ce.at[s, sister], os.at[s], orr.at[s], at(0, 0, 0, sister))

    def send_motion(m):
        return copy(mo.at[m], mo_in.at[m], ms.at[m], mr.at[m], at(0, 0, RING[m], core))

    def send_pre(s):
        return copy(ldp.at[s, sister], pre.at[s], ps.at[s], pr.at[s], at(0, 0, 0, sister))

    def send_loads(s):
        return copy(ldp.at[s, core], ld_in.at[s], ls.at[s], lr.at[s], plus(s, core))

    def send_loads_across(s):
        q = s - GROUP * len(MERGED)
        return copy(ldp.at[s, sister], ld_other.at[q], qs.at[q], qr.at[q], plus(s, sister))

    slots = [range(GROUP * c, GROUP * (c + 1)) for c in range(len(PLANE) // GROUP)]
    straight = slots[0]

    local = [
        pltpu.make_async_copy(center, raw, own.at[0]),
        pltpu.make_async_copy(fluid, fl.at[0], own.at[1]),
        pltpu.make_async_copy(poly, pv, own.at[2]),
    ]
    for c in local:
        c.start()
    barrier = pltpu.get_barrier_semaphore()
    greeted = [at(0, 0, RING[m], core) for m in range(1, Z)]
    greeted += [plus(s, core) for s in range(OWN)]
    greeted += [plus(s, sister) for s in straight]
    greeted += [minus(s, sister) for s in range(GROUP * len(MERGED), OWN + 1)]
    for where in greeted:
        pl.semaphore_signal(barrier, inc=1, device_id=where, device_id_type=MESH)
    for c in local:
        c.wait()
    coef = raw[3:, :] * TOP
    places = raw[0:8, :] * float(WAVES)
    ce[OWN, core, 0:half] = jnp.concatenate([coef[:half], coef[half:]], axis=1)
    ce[OWN, core, half:] = jnp.concatenate([places, places], axis=1)
    left = lax.broadcasted_iota(jnp.int32, (half, wide), 1) < wc
    left8 = lax.broadcasted_iota(jnp.int32, (8, wide), 1) < wc
    pl.semaphore_wait(barrier, len(greeted))
    send_fluid(1).start()
    for s in straight:
        send_center(s).start()
        send_across(s).start()
    for m in range(2, Z):
        send_fluid(m).start()
    send_across(OWN).start()
    for s in range(len(straight), OWN):
        send_center(s).start()

    def ready_center(c):
        for j, s in enumerate(slots[c]):
            a, b = ce[s, 0, 0:half], ce[s, 1, 0:half]
            upper = jnp.where(left, a, pltpu.roll(b, wc, 1))
            lower = jnp.where(left, pltpu.roll(a, wc, 1), b)
            high, low = split(jnp.concatenate([upper, lower], axis=0))
            part = pl.ds(j * wide, wide)
            chl[c, 0:n, part] = high
            chl[c, n:, part] = low
            spots = jnp.transpose(jnp.where(left8, ce[s, 0, half:], ce[s, 1, half:]))
            for a in range(3):
                cp[c, a, part, :] = jnp.broadcast_to(spots[:, a : a + 1], (wide, 128))

    def ready_fluid(p):
        for h in range(2):
            m = 2 * p + h
            part = pl.ds(h * wf, wf)
            high, low = split(fl[m, 3:, :] * TOP)
            fhl[p, 0:n, part] = high
            fhl[p, n:, part] = low
            fx[p, :, part] = fl[m, 0:8, :] * float(WAVES)

    def values(c, p, slot):
        for h in range(2):
            part = pl.ds(h * wf, wf)
            px, py, pz = (fx[p, a : a + 1, part] for a in range(3))
            for j in range(0, GROUP * wide, step_rows):
                rows = pl.ds(j, step_rows)
                dx, dy, dz = cp[c, 0, rows, :] - px, cp[c, 1, rows, :] - py, cp[c, 2, rows, :] - pz
                sq = dx * dx + dy * dy + dz * dz
                inv = lax.rsqrt(sq)
                turns = sq * inv
                f = turns - jnp.round(turns)
                size = jnp.abs(f)
                rest = 0.5 - size
                q = size * rest
                value = (f * rest * inv) * ((q + MID) * q + LOW)
                high, low = split(value)
                kh[slot, rows, part] = high
                kl[slot, rows, part] = low

    seen_c, seen_p = set(), set()

    def sums(c, p, slot):
        k_high, k_low = kh[slot], kl[slot]
        across = ((1,), (0,))
        both = dot(chl[c], k_high, across)
        out = both[:n] + both[n:] + dot(chl[c, 0:n], k_low, across)
        for h in range(2):
            piece = out[:, h * wf : (h + 1) * wf]
            mo[2 * p + h] = mo[2 * p + h] + piece if p in seen_p else piece
        back = ((1,), (1,))
        both = dot(fhl[p], k_high, back)
        out = both[:n] + both[n:] + dot(fhl[p, 0:n], k_low, back)
        ld[c] = ld[c] + out if c in seen_c else out
        seen_c.add(c)
        seen_p.add(p)

    def pack(c):
        for j, s in enumerate(slots[c]):
            part = pl.ds(j * wide, wide)
            upper, lower = ld[c, 0:half, part], ld[c, half:, part]
            ldp[s, 0] = jnp.where(left, upper, pltpu.roll(lower, wc, 1))
            ldp[s, 1] = jnp.where(left, pltpu.roll(upper, wc, 1), lower)

    def finished(k):
        c, p = ORDER[k]
        if all(o[1] != p for o in ORDER[k + 1 :]):
            for m in (2 * p + 1, 2 * p):
                if m:
                    send_motion(m).start()
        if all(o[0] != c for o in ORDER[k + 1 :]):
            pack(c)
            for s in slots[c]:
                if c in MERGED:
                    send_pre(s).start()
                else:
                    if s != OWN:
                        send_loads(s).start()
                    send_loads_across(s).start()
        if k and ORDER[k - 1][0] in MERGED and ORDER[k - 1][0] != c:
            for s in slots[ORDER[k - 1][0]]:
                send_pre(s).wait_recv()
                ldp[s, core] = ldp[s, core] + pre[s]
                send_loads(s).start()

    arrived_c, arrived_p = set(), set()
    handed = {1: 1, 2: 2, 3: 3}
    for k, (c, p) in enumerate(ORDER):
        if p not in arrived_p:
            for m in (2 * p, 2 * p + 1):
                if m:
                    send_fluid(m).wait_recv()
            ready_fluid(p)
            arrived_p.add(p)
        if k in handed:
            for s in slots[handed[k]]:
                if s != OWN:
                    send_center(s).wait_recv()
                    hand_on(s).start()
        if c not in arrived_c:
            for s in slots[c]:
                if s in straight:
                    send_center(s).wait_recv()
                from_other(s).wait_recv()
            ready_center(c)
            arrived_c.add(c)
        if k:
            sums(*ORDER[k - 1], (k - 1) % 2)
        values(c, p, k % 2)
        if k:
            finished(k - 1)
    last = len(ORDER) - 1
    sums(*ORDER[last], last % 2)
    finished(last)

    total = mo[0]
    affine = jnp.transpose(pv[...])
    for a in range(3):
        total = total + affine[:, a + 1 : a + 2] * fl[0, a : a + 1, :]
    total = total + affine[:, 0:1]
    for m in range(Z - 1, 0, -1):
        send_motion(m).wait_recv()
        total = total + mo_in[m]
    motion[...] = total
    total = ldp[OWN, core]
    for s in range(OWN):
        send_loads(s).wait_recv()
        total = total + ld_in[s]
    for s in range(GROUP * len(MERGED), OWN + 1):
        send_loads_across(s).wait_recv()
        total = total + ld_other[s - GROUP * len(MERGED)]
    loads[0:half, :] = total[:, :wc]
    loads[half:, :] = total[:, wc:]
    for m in range(1, Z):
        send_fluid(m).wait_send()
        send_motion(m).wait_send()
    for s in range(OWN + 1):
        if s != OWN:
            send_center(s).wait_send()
            send_loads(s).wait_send()
        (send_across(s) if s in straight or s == OWN else hand_on(s)).wait_send()
        if s < GROUP * len(MERGED):
            send_pre(s).wait_send()
        else:
            send_loads_across(s).wait_send()


def per_device(fluid_data, center_data, poly_coef):
    f32, bf16 = jnp.float32, jnp.bfloat16
    height, wf = fluid_data.shape
    wc = center_data.shape[1]
    n = height - 3
    slots, cols, rows = len(PLANE), len(PLANE) // GROUP, Z // 2
    deep, broad = GROUP * CORES * wc, 2 * wf
    merged = GROUP * len(MERGED)
    vmem = pl.BlockSpec(memory_space=pltpu.VMEM)
    hbm = pl.BlockSpec(memory_space=pltpu.HBM)
    counts = (3, Z, Z, slots, slots, slots, slots, Z, Z, merged, merged, slots, slots, slots - merged, slots - merged)
    return pl.pallas_call(
        body,
        out_shape=(jax.ShapeDtypeStruct((n, wf), f32), jax.ShapeDtypeStruct((n, wc), f32)),
        in_specs=[hbm] * 3,
        out_specs=(vmem, vmem),
        scratch_shapes=[
            pltpu.VMEM((Z, height, wf), f32),
            pltpu.VMEM((height, wc), f32),
            pltpu.VMEM((slots, CORES, n // 2 + 8, 2 * wc), f32),
            pltpu.VMEM((4, n), f32),
            pltpu.VMEM((cols, 3, deep, 128), f32),
            pltpu.VMEM((cols, 2 * n, deep), bf16),
            pltpu.VMEM((rows, 2 * n, broad), bf16),
            pltpu.VMEM((rows, 8, broad), f32),
            pltpu.VMEM((2, deep, broad), bf16),
            pltpu.VMEM((2, deep, broad), bf16),
            pltpu.VMEM((Z, n, wf), f32),
            pltpu.VMEM((Z, n, wf), f32),
            pltpu.VMEM((cols, n, deep), f32),
            pltpu.VMEM((slots, CORES, n // 2, 2 * wc), f32),
            pltpu.VMEM((merged, n // 2, 2 * wc), f32),
            pltpu.VMEM((slots, n // 2, 2 * wc), f32),
            pltpu.VMEM((slots - merged, n // 2, 2 * wc), f32),
            *[pltpu.SemaphoreType.DMA((k,)) for k in counts],
        ],
        compiler_params=pltpu.CompilerParams(
            collective_id=0, has_side_effects=True, vmem_limit_bytes=67_043_328
        ),
    )(fluid_data, center_data, poly_coef.T)


def solution(mesh):
    return jax.shard_map(
        per_device,
        mesh=mesh,
        in_specs=(P(None, ("row", "col")), P(None, ("col", "row")), P()),
        out_specs=(P(None, ("row", "col")), P(None, ("col", "row"))),
        check_vma=False,
    )
```

time: 71.2 us -> 37.5 us (0.53)
  the two profiles are of different devices: /device:TPU:32 before, /device:TPU:1 now
where the time goes in v2:
time: 37.5 us; the launch traced here: 37.2 us
  Pallas kernels  34.6 us (92%)
  local copies, waits for them, and re-layouts  1.96 us (5%)
  between operations  0.65 us (2%)
    pallas_call x1, Pallas kernels, per_device(): pl.pallas_call(body, out_shape=(jax.ShapeDtypeStruct((n, wf), f32), jax.S...  34.6 us
    unnamed x4, local copies, waits for them, and re-layouts  1.96 us

profile of v2, /device:TPU:1, one launch (start us, length us, event | category | flops | bytes accessed | tf_op | source)
XLA Modules:
  0.0 37.2 jit_solution(10904753841830816646)
XLA Ops:
  0.6 34.6 %shard_map.50 = (f32[48,128]{1,0:T(8,128)}, f32[48,64]{1,0:T(8,128)}) custom-call(f32[51,128]{1,0:T(8,128)} %fluid.1, f32[51,64]{1,0:T(8,128)} %center.1, f32[4,48]{1,0:T(4,128)} %bitcast.1), custom_call_target="tpu_custom_call" | custom-call | tf_op jit(solution)/shard_map/pallas_call | solution.py:295
  35.3 0.0 copy-start
  35.3 1.4 %copy.7 = f32[48,128]{1,0:T(8,128)} copy(f32[48,128]{1,0:T(8,128)} %get-tuple-element.4) | data formatting | bytes 49152
  36.6 0.0 copy-done
  36.6 0.6 %copy.8 = f32[48,64]{1,0:T(8,128)} copy(f32[48,64]{1,0:T(8,128)S(1)} %copy-done) | data formatting | bytes 24576
Async XLA Ops:
  35.3 1.4 %copy-start = (f32[48,64]{1,0:T(8,128)S(1)}, f32[48,64]{1,0:T(8,128)}, u32[]{:S(2)}) copy-start(f32[48,64]{1,0:T(8,128)} %get-tuple-element.5) | copy-start | bytes 36868

commit v3 on v2

--- a/solution.py
+++ b/solution.py
@@ -16,14 +16,20 @@
 GROUP = 4
 PLANE = (
     ((1, 0), (3, 0), (0, 1), (0, 3))
-    + ((2, 2), (2, 1), (2, 3), (1, 2))
-    + ((3, 2), (1, 3), (3, 1), (3, 3))
-    + ((2, 0), (0, 2), (1, 1), (0, 0))
+    + ((1, 1), (1, 3), (3, 1), (3, 3))
+    + ((2, 3), (1, 2), (3, 2), (2, 2))
+    + ((2, 1), (2, 0), (0, 2), (0, 0))
 )
 OWN = len(PLANE) - 1
 RING = (0, 1, 7, 2, 6, 3, 5, 4)
-ORDER = tuple((c, p) for c in (0, 1) for p in range(4)) + tuple((c, p) for p in (3, 2, 1, 0) for c in (2, 3))
-MERGED = (0, 1)
+ORDER = (
+    ((0, 0), (0, 1), (1, 0), (1, 1), (0, 2), (1, 2), (2, 2), (3, 2))
+    + ((0, 3), (1, 3), (2, 3), (3, 3), (2, 1), (2, 0), (3, 1), (3, 0))
+)
+STRAIGHT = (0, 1)
+HANDED = {3: 2, 4: 3}
+READY = {0: 0, 2: 1, 5: 2, 6: 3}
+MERGED = (0, 1, 2)
 
 
 def dot(a, b, dims):
@@ -98,7 +104,7 @@
         return copy(ldp.at[s, sister], ld_other.at[q], qs.at[q], qr.at[q], plus(s, sister))
 
     slots = [range(GROUP * c, GROUP * (c + 1)) for c in range(len(PLANE) // GROUP)]
-    straight = slots[0]
+    straight = [s for c in STRAIGHT for s in slots[c]]
 
     local = [
         pltpu.make_async_copy(center, raw, own.at[0]),
@@ -198,13 +204,16 @@
             ldp[s, 0] = jnp.where(left, upper, pltpu.roll(lower, wc, 1))
             ldp[s, 1] = jnp.where(left, pltpu.roll(upper, wc, 1), lower)
 
+    merging = []
+
     def finished(k):
         c, p = ORDER[k]
         if all(o[1] != p for o in ORDER[k + 1 :]):
             for m in (2 * p + 1, 2 * p):
                 if m:
                     send_motion(m).start()
-        if all(o[0] != c for o in ORDER[k + 1 :]):
+        done = all(o[0] != c for o in ORDER[k + 1 :])
+        if done:
             pack(c)
             for s in slots[c]:
                 if c in MERGED:
@@ -213,14 +222,13 @@
                     if s != OWN:
                         send_loads(s).start()
                     send_loads_across(s).start()
-        if k and ORDER[k - 1][0] in MERGED and ORDER[k - 1][0] != c:
-            for s in slots[ORDER[k - 1][0]]:
-                send_pre(s).wait_recv()
-                ldp[s, core] = ldp[s, core] + pre[s]
-                send_loads(s).start()
-
-    arrived_c, arrived_p = set(), set()
-    handed = {1: 1, 2: 2, 3: 3}
+        for s in merging:
+            send_pre(s).wait_recv()
+            ldp[s, core] = ldp[s, core] + pre[s]
+            send_loads(s).start()
+        merging[:] = slots[c] if done and c in MERGED else ()
+
+    arrived_p = set()
     for k, (c, p) in enumerate(ORDER):
         if p not in arrived_p:
             for m in (2 * p, 2 * p + 1):
@@ -228,18 +236,17 @@
                     send_fluid(m).wait_recv()
             ready_fluid(p)
             arrived_p.add(p)
-        if k in handed:
-            for s in slots[handed[k]]:
+        if k in HANDED:
+            for s in slots[HANDED[k]]:
                 if s != OWN:
                     send_center(s).wait_recv()
                     hand_on(s).start()
-        if c not in arrived_c:
-            for s in slots[c]:
+        if k in READY:
+            for s in slots[READY[k]]:
                 if s in straight:
                     send_center(s).wait_recv()
                 from_other(s).wait_recv()
-            ready_center(c)
-            arrived_c.add(c)
+            ready_center(READY[k])
         if k:
             sums(*ORDER[k - 1], (k - 1) % 2)
         values(c, p, k % 2)

time: 37.5 us -> 36.9 us (0.984)
  Pallas kernels: 34.6 us -> 34.1 us
    pallas_call x1, Pallas kernels: 34.6 us -> 34.1 us  [per_device(): pl.pallas_call(body, out_shape=(jax.ShapeDtypeStruct((n, wf), f32), jax.S...]
where the time goes in v3:
time: 36.9 us; the launch traced here: 36.7 us
  Pallas kernels  34.1 us (92%)
  local copies, waits for them, and re-layouts  1.96 us (5%)
  between operations  0.65 us (2%)
    pallas_call x1, Pallas kernels, per_device(): pl.pallas_call(body, out_shape=(jax.ShapeDtypeStruct((n, wf), f32), jax.S...  34.1 us
    unnamed x4, local copies, waits for them, and re-layouts  1.96 us

profile of v3, /device:TPU:1, one launch (start us, length us, event | category | flops | bytes accessed | tf_op | source)
XLA Modules:
  0.0 36.7 jit_solution(12967092516677607361)
XLA Ops:
  0.6 34.1 %shard_map.50 = (f32[48,128]{1,0:T(8,128)}, f32[48,64]{1,0:T(8,128)}) custom-call(f32[51,128]{1,0:T(8,128)} %fluid.1, f32[51,64]{1,0:T(8,128)} %center.1, f32[4,48]{1,0:T(4,128)} %bitcast.1), custom_call_target="tpu_custom_call" | custom-call | tf_op jit(solution)/shard_map/pallas_call | solution.py:302
  34.7 0.0 copy-start
  34.7 1.4 %copy.7 = f32[48,128]{1,0:T(8,128)} copy(f32[48,128]{1,0:T(8,128)} %get-tuple-element.4) | data formatting | bytes 49152
  36.1 0.0 copy-done
  36.1 0.6 %copy.8 = f32[48,64]{1,0:T(8,128)} copy(f32[48,64]{1,0:T(8,128)S(1)} %copy-done) | data formatting | bytes 24576
Async XLA Ops:
  34.7 1.4 %copy-start = (f32[48,64]{1,0:T(8,128)S(1)}, f32[48,64]{1,0:T(8,128)}, u32[]{:S(2)}) copy-start(f32[48,64]{1,0:T(8,128)} %get-tuple-element.5) | copy-start | bytes 36868

commit v4 on v3

--- a/solution.py
+++ b/solution.py
@@ -42,9 +42,23 @@
     return high, low
 
 
-def body(fluid, center, poly, motion, loads, *scratch):
-    fl, raw, ce, pv, cp, chl, fhl, fx, kh, kl, mo, mo_in, ld, ldp, pre, ld_in, ld_other = scratch[:17]
-    own, fs, fr, cs, cr, os, orr, ms, mr, ps, pr, ls, lr, qs, qr = scratch[17:]
+def body(*refs):
+    n, wf = refs[3].shape
+    wc = refs[1].shape[1]
+    deep, broad = GROUP * CORES * wc, 2 * wf
+    pl.run_scoped(
+        functools.partial(work, *refs),
+        pltpu.VMEM((len(PLANE) // GROUP, 2 * n, deep), jnp.bfloat16),
+        pltpu.VMEM((Z // 2, 2 * n, broad), jnp.bfloat16),
+        pltpu.VMEM((2, deep, broad), jnp.bfloat16),
+        pltpu.VMEM((2, deep, broad), jnp.bfloat16),
+    )
+
+
+def work(fluid, center, poly, motion, loads, *scratch):
+    fl, raw, ce, pv, cp, fx, mo, mo_in, ld, ldp, pre, ld_in, ld_other = scratch[:13]
+    own, fs, fr, cs, cr, os, orr, ms, mr, ps, pr, ls, lr, qs, qr = scratch[13:28]
+    chl, fhl, kh, kl = scratch[28:]
     row, col = lax.axis_index("row"), lax.axis_index("col")
     y, z, core = row // 4, ((row // 2) % 2) * 4 + col // 4, row % 2
     x = col % 4
@@ -289,7 +303,7 @@
 
 
 def per_device(fluid_data, center_data, poly_coef):
-    f32, bf16 = jnp.float32, jnp.bfloat16
+    f32 = jnp.float32
     height, wf = fluid_data.shape
     wc = center_data.shape[1]
     n = height - 3
@@ -310,11 +324,7 @@
             pltpu.VMEM((slots, CORES, n // 2 + 8, 2 * wc), f32),
             pltpu.VMEM((4, n), f32),
             pltpu.VMEM((cols, 3, deep, 128), f32),
-            pltpu.VMEM((cols, 2 * n, deep), bf16),
-            pltpu.VMEM((rows, 2 * n, broad), bf16),
             pltpu.VMEM((rows, 8, broad), f32),
-            pltpu.VMEM((2, deep, broad), bf16),
-            pltpu.VMEM((2, deep, broad), bf16),
             pltpu.VMEM((Z, n, wf), f32),
             pltpu.VMEM((Z, n, wf), f32),
             pltpu.VMEM((cols, n, deep), f32),

time: 36.9 us -> 36.4 us (0.986)
  Pallas kernels: 34.1 us -> 33.6 us
    pallas_call x1, Pallas kernels: 34.1 us -> 33.6 us  [per_device(): pl.pallas_call(body, out_shape=(jax.ShapeDtypeStruct((n, wf), f32), jax.S...]
where the time goes in v4:
time: 36.4 us; the launch traced here: 36.2 us
  Pallas kernels  33.6 us (92%)
  local copies, waits for them, and re-layouts  1.96 us (5%)
  between operations  0.65 us (2%)
    pallas_call x1, Pallas kernels, per_device(): pl.pallas_call(body, out_shape=(jax.ShapeDtypeStruct((n, wf), f32), jax.S...  33.6 us
    unnamed x4, local copies, waits for them, and re-layouts  1.96 us

profile of v4, /device:TPU:1, one launch (start us, length us, event | category | flops | bytes accessed | tf_op | source)
XLA Modules:
  0.0 36.2 jit_solution(16812195720718629193)
XLA Ops:
  0.6 33.6 %shard_map.50 = (f32[48,128]{1,0:T(8,128)}, f32[48,64]{1,0:T(8,128)}) custom-call(f32[51,128]{1,0:T(8,128)} %refs_0_.1, f32[51,64]{1,0:T(8,128)} %refs_1_.1, f32[4,48]{1,0:T(4,128)} %bitcast.1), custom_call_target="tpu_custom_call" | custom-call | tf_op jit(solution)/shard_map/pallas_call | solution.py:316
  34.2 0.0 copy-start
  34.2 1.4 %copy.7 = f32[48,128]{1,0:T(8,128)} copy(f32[48,128]{1,0:T(8,128)} %get-tuple-element.4) | data formatting | bytes 49152
  35.6 0.0 copy-done
  35.6 0.6 %copy.8 = f32[48,64]{1,0:T(8,128)} copy(f32[48,64]{1,0:T(8,128)S(1)} %copy-done) | data formatting | bytes 24576
Async XLA Ops:
  34.2 1.4 %copy-start = (f32[48,64]{1,0:T(8,128)S(1)}, f32[48,64]{1,0:T(8,128)}, u32[]{:S(2)}) copy-start(f32[48,64]{1,0:T(8,128)} %get-tuple-element.5) | copy-start | bytes 36868

commit v5 on v4

--- a/solution.py
+++ b/solution.py
@@ -17,8 +17,8 @@
 PLANE = (
     ((1, 0), (3, 0), (0, 1), (0, 3))
     + ((1, 1), (1, 3), (3, 1), (3, 3))
-    + ((2, 3), (1, 2), (3, 2), (2, 2))
-    + ((2, 1), (2, 0), (0, 2), (0, 0))
+    + ((2, 1), (2, 3), (1, 2), (2, 2))
+    + ((3, 2), (2, 0), (0, 2), (0, 0))
 )
 OWN = len(PLANE) - 1
 RING = (0, 1, 7, 2, 6, 3, 5, 4)
@@ -30,6 +30,8 @@
 HANDED = {3: 2, 4: 3}
 READY = {0: 0, 2: 1, 5: 2, 6: 3}
 MERGED = (0, 1, 2)
+SENT = {8: (7,), 10: (8, 9), 12: (10, 11), 14: (12, 13), 15: (14,)}
+SUMMED = {12: (0, 1), 15: (2,)}
 
 
 def dot(a, b, dims):
@@ -218,16 +220,13 @@
             ldp[s, 0] = jnp.where(left, upper, pltpu.roll(lower, wc, 1))
             ldp[s, 1] = jnp.where(left, pltpu.roll(upper, wc, 1), lower)
 
-    merging = []
-
     def finished(k):
         c, p = ORDER[k]
         if all(o[1] != p for o in ORDER[k + 1 :]):
             for m in (2 * p + 1, 2 * p):
                 if m:
                     send_motion(m).start()
-        done = all(o[0] != c for o in ORDER[k + 1 :])
-        if done:
+        if all(o[0] != c for o in ORDER[k + 1 :]):
             pack(c)
             for s in slots[c]:
                 if c in MERGED:
@@ -236,11 +235,12 @@
                     if s != OWN:
                         send_loads(s).start()
                     send_loads_across(s).start()
-        for s in merging:
+
+    def merge(c):
+        for s in slots[c]:
             send_pre(s).wait_recv()
             ldp[s, core] = ldp[s, core] + pre[s]
             send_loads(s).start()
-        merging[:] = slots[c] if done and c in MERGED else ()
 
     arrived_p = set()
     for k, (c, p) in enumerate(ORDER):
@@ -264,12 +264,25 @@
         if k:
             sums(*ORDER[k - 1], (k - 1) % 2)
         values(c, p, k % 2)
-        if k:
-            finished(k - 1)
+        for done in SENT.get(k, ()):
+            finished(done)
+        for done in SUMMED.get(k, ()):
+            merge(done)
     last = len(ORDER) - 1
     sums(*ORDER[last], last % 2)
     finished(last)
 
+    for m in range(1, Z):
+        send_fluid(m).wait_send()
+        if m > 3:
+            send_motion(m).wait_send()
+    for s in range(OWN + 1):
+        if s != OWN:
+            send_center(s).wait_send()
+        (send_across(s) if s in straight or s == OWN else hand_on(s)).wait_send()
+        if s not in slots[-1]:
+            send_pre(s).wait_send()
+            send_loads(s).wait_send()
     total = mo[0]
     affine = jnp.transpose(pv[...])
     for a in range(3):
@@ -288,18 +301,12 @@
         total = total + ld_other[s - GROUP * len(MERGED)]
     loads[0:half, :] = total[:, :wc]
     loads[half:, :] = total[:, wc:]
-    for m in range(1, Z):
-        send_fluid(m).wait_send()
+    for m in (1, 2, 3):
         send_motion(m).wait_send()
-    for s in range(OWN + 1):
+    for s in slots[-1]:
         if s != OWN:
-            send_center(s).wait_send()
             send_loads(s).wait_send()
-        (send_across(s) if s in straight or s == OWN else hand_on(s)).wait_send()
-        if s < GROUP * len(MERGED):
-            send_pre(s).wait_send()
-        else:
-            send_loads_across(s).wait_send()
+        send_loads_across(s).wait_send()
 
 
 def per_device(fluid_data, center_data, poly_coef):

time: 36.4 us -> 35.8 us (0.984)
  Pallas kernels: 33.6 us -> 33 us
    pallas_call x1, Pallas kernels: 33.6 us -> 33 us  [per_device(): pl.pallas_call(body, out_shape=(jax.ShapeDtypeStruct((n, wf), f32), jax.S...]
where the time goes in v5:
time: 35.8 us; the launch traced here: 35.6 us
  Pallas kernels  33 us (92%)
  local copies, waits for them, and re-layouts  1.96 us (5%)
  between operations  0.65 us (2%)
    pallas_call x1, Pallas kernels, per_device(): pl.pallas_call(body, out_shape=(jax.ShapeDtypeStruct((n, wf), f32), jax.S...  33 us
    unnamed x4, local copies, waits for them, and re-layouts  1.96 us

profile of v5, /device:TPU:1, one launch (start us, length us, event | category | flops | bytes accessed | tf_op | source)
XLA Modules:
  0.0 35.6 jit_solution(5947930102875244149)
XLA Ops:
  0.6 33.0 %shard_map.50 = (f32[48,128]{1,0:T(8,128)}, f32[48,64]{1,0:T(8,128)}) custom-call(f32[51,128]{1,0:T(8,128)} %refs_0_.1, f32[51,64]{1,0:T(8,128)} %refs_1_.1, f32[4,48]{1,0:T(4,128)} %bitcast.1), custom_call_target="tpu_custom_call" | custom-call | tf_op jit(solution)/shard_map/pallas_call | solution.py:323
  33.7 0.0 copy-start
  33.7 1.4 %copy.7 = f32[48,128]{1,0:T(8,128)} copy(f32[48,128]{1,0:T(8,128)} %get-tuple-element.4) | data formatting | bytes 49152
  35.0 0.0 copy-done
  35.0 0.6 %copy.8 = f32[48,64]{1,0:T(8,128)} copy(f32[48,64]{1,0:T(8,128)S(1)} %copy-done) | data formatting | bytes 24576
Async XLA Ops:
  33.7 1.4 %copy-start = (f32[48,64]{1,0:T(8,128)S(1)}, f32[48,64]{1,0:T(8,128)}, u32[]{:S(2)}) copy-start(f32[48,64]{1,0:T(8,128)} %get-tuple-element.5) | copy-start | bytes 36868
